TPU v7x, 512 devices: a whole 4x4x16 slice. The times are simulated.
512 devices in a mesh: ctx: 128 (over z, x, y_hi), head: 4 (over y_lo, core).
Axes of the slice: x: 4, y: 4 (y_hi: 2, y_lo: 2; y = y_hi * 2 + y_lo), z: 16, core: 2. Of those that a mesh axis runs over, the one named last changes fastest.
Arguments:
- queries: bfloat16 [8192, 8192], P('ctx', 'head'), may hold values from -6 to 6
- keys: bfloat16 [8192, 128], P('ctx'), may hold values from -6 to 6
- key_gain: float32 [128], replicated, may hold values from 0.25 to 1.75
- key_bias: float32 [128], replicated, may hold values from -0.5 to 0.5
- head_weights: bfloat16 [8192, 64], P('ctx', 'head'), may hold values from -6 to 6
- positions: int32 [8192], P('ctx'), may hold values from 0 to 6143, as said below
Outputs:
- index_scores: float32 [8192, 8192], P(('ctx', 'head'))
Inputs may be any that keep to these rules, and one draw needn't show every extreme that they name: `positions`: positions of packed documents: the first 6144 tokens form one document and the rest is split into one to three documents at drawn points; a token's position counts from its document's first token.
All inputs are finite; a program needn't handle non-finite values.
Results may differ from a plain program's by a relative error of at most 0.0095.
Values may be sent and summed in bfloat16 or wider, within the bound.
No kernel may reach another device: no remote copies, remote signals or barrier semaphores. Data moves between devices by JAX's collectives and lax.ppermute only.
A program may use at most 64 MiB of HBM per device.

v0:
```python
import math
import jax
import jax.numpy as jnp
import numpy as np
from jax import lax
from jax.sharding import PartitionSpec as P

H = 64
DH = 128
ROPE = 64


def yarn_frequencies(rope_dims):
    half_dims = rope_dims // 2
    exponent = np.arange(0, rope_dims, 2) / rope_dims
    extra_freq = 1.0 / 10000.0**exponent
    inter_freq = extra_freq / 40.0

    def correction(beta):
        return rope_dims * math.log(4096.0 / (beta * 2.0 * math.pi)) / (2.0 * math.log(10000.0))

    low_dim = max(math.floor(correction(32.0)), 0)
    high_dim = min(math.ceil(correction(1.0)), rope_dims - 1)
    ramp_values = np.clip((np.arange(half_dims) - low_dim) / (high_dim - low_dim), 0.0, 1.0)
    return (inter_freq * ramp_values + extra_freq * (1.0 - ramp_values)).astype(np.float32)


def rotate(values, angles):
    half_rope = ROPE // 2
    cosine = jnp.cos(angles)[:, None, :]
    sine = jnp.sin(angles)[:, None, :]
    first = values[..., :half_rope]
    second = values[..., half_rope:ROPE]
    return jnp.concatenate(
        [first * cosine - second * sine, second * cosine + first * sine, values[..., ROPE:]], -1
    )


def key_norm(keys, key_gain, key_bias):
    values = keys.astype(jnp.float32)
    centered = values - jnp.mean(values, axis=-1, keepdims=True)
    spread = jnp.mean(centered * centered, axis=-1, keepdims=True)
    return centered * lax.rsqrt(spread + 1e-06) * key_gain + key_bias


def tile_scores(q_block, weights, k_block, groups, row_glob, row_doc, key_glob):
    rows_here = q_block.shape[0]
    heads_here = weights.shape[1]
    raw = lax.dot_general(
        q_block.reshape(rows_here * heads_here, DH),
        k_block,
        (((1,), (1,)), ((), ())),
        preferred_element_type=jnp.float32,
    )
    active = jnp.maximum(raw, 0.0).reshape(
        rows_here, groups, heads_here // groups, k_block.shape[0]
    )
    partial_sum = jnp.sum(
        active * weights.reshape(rows_here, groups, heads_here // groups, 1), axis=2
    )
    visible = (key_glob[None, :] >= row_doc[:, None]) & (key_glob[None, :] <= row_glob[:, None])
    partial_sum = jnp.where(visible[:, None, :], partial_sum, jnp.zeros_like(partial_sum))
    return partial_sum.astype(jnp.bfloat16)


def on_device(queries, keys, key_gain, key_bias, head_weights, positions):
    tok_rows = queries.shape[0]
    local_heads = queries.shape[1] // DH
    ctx_rank = lax.axis_index("ctx")
    freqs = jnp.asarray(yarn_frequencies(ROPE))
    angles = positions.astype(jnp.float32)[:, None] * freqs[None, :]
    q_rot = (
        rotate(queries.astype(jnp.float32).reshape(tok_rows, local_heads, DH), angles)
        .reshape(tok_rows, local_heads * DH)
        .astype(jnp.bfloat16)
    )
    k_rot = (
        rotate(key_norm(keys, key_gain, key_bias)[:, None, :], angles)
        .reshape(tok_rows, DH)
        .astype(jnp.bfloat16)
    )
    scale = 1.0 / math.sqrt(H * DH)
    groups = 1
    rows_w = head_weights.astype(jnp.float32) * scale
    row_glob = ctx_rank * tok_rows + jnp.arange(tok_rows, dtype=jnp.int32)
    row_doc = row_glob - positions
    rows_here = q_rot.shape[0]
    out_type = jnp.bfloat16
    row_last = jnp.max(row_glob)
    doc_first = jnp.min(row_doc)

    def score_block(k_block, key_glob):
        parts = tile_scores(q_rot, rows_w, k_block, groups, row_glob, row_doc, key_glob)
        return parts[:, 0, :]

    piece = lax.all_gather(k_rot, "ctx", axis=0, tiled=True)
    start = jnp.int32(0)
    piece_len = piece.shape[0]
    block_len = math.gcd(piece_len, 512)
    count = piece_len // block_len

    def compute(operand):
        stacked = piece.reshape(count, block_len, DH)
        offsets = block_len * jnp.arange(count, dtype=jnp.int32)

        def one_block(inputs):
            k_block, offset = inputs
            return score_block(k_block, offset + jnp.arange(block_len, dtype=jnp.int32))

        tiles = lax.map(one_block, (stacked, offsets))
        return jnp.transpose(tiles, (1, 0, 2)).reshape(rows_here, piece_len)

    def skip(operand):
        return jnp.zeros((rows_here, piece_len), out_type)

    live = (start <= row_last) & (start + piece_len > doc_first)
    partials = lax.cond(live, compute, skip, 0)
    return lax.psum_scatter(partials, "head", scatter_dimension=0, tiled=True).astype(jnp.float32)


def solution(mesh):
    in_specs = (P("ctx", "head"), P("ctx", None), P(), P(), P("ctx", "head"), P("ctx"))
    out_specs = P(("ctx", "head"), None)
    return jax.shard_map(
        on_device, mesh=mesh, in_specs=in_specs, out_specs=out_specs, check_vma=False
    )
```

profile of v0, /device:TPU:1, one launch (start us, length us, event | category | flops | bytes accessed | tf_op | source)
XLA Modules:
  0.0 366.6 jit_solution(11451459381095986542)
XLA Ops:
  14.6 207.3 %all-gather.3.cloned.1.call-done = bf16[8192,1,128]{2,0,1:T(8,128)(2,1)} async-done(((bf16[64,1,128]{2,0,1:T(8,128)(2,1)}), bf16[8192,1,128]{2,0,1:T(8,128)(2,1)}) %all-gather.3.cloned.1.call-update) | async-done | bytes 2097168 | tf_op jit(solution)/shard_map/all_gather | solution.py:96
  221.9 102.7 %conditional.1 = (bf16[64,8192]{1,0:T(8,128)(2,1)S(1)}) conditional(s32[]{:T(128)} %convert_element_type.40, () %tuple.18, (bf16[8192,128]{1,0:T(8,128)(2,1)}, bf16[64,16,128]{2,1,0:T(8,128)(2,1)S(1)}, f32[64,16]{1,0:T(8,128)S(1)}, s32[64]{0:T(128)S(1)}, s32[64]{0:T(128)S(1)}) %tuple.49), branch_computations={%region_4.0_spmd, %region_5.9_spmd} | conditional | flops 135890448 | bytes 13190965 | solution.py:117
  222.6 101.8 %while.13 = (s32[]{:T(128)}, bf16[16,64,512]{2,1,0:T(8,128)(2,1)S(1)}, s32[16]{0:T(128)S(1)}, s32[64]{0:T(128)S(1)}, s32[64]{0:T(128)S(1)}, /*index=5*/bf16[16,5...) while((s32[]{:T(128)}, ...), condition=%wide.wide.region_8.8_spmd, body=%wide.wide.region_6.7_spmd.sunk | while | flops 135889408 | bytes 8988281 | solution.py:110
  222.6 2.6 maximum_bitcast_fusion.3
  225.3 1.9 copy.30
  229.0 2.6 maximum_bitcast_fusion.3
  231.6 1.9 copy.30
  235.4 2.6 maximum_bitcast_fusion.3
  238.0 1.9 copy.30
  241.7 2.6 maximum_bitcast_fusion.3
  248.1 2.6 maximum_bitcast_fusion.3
  250.7 1.9 copy.30
  254.5 2.6 maximum_bitcast_fusion.3
  260.8 2.6 maximum_bitcast_fusion.3
  267.2 2.6 maximum_bitcast_fusion.3
  273.6 2.6 maximum_bitcast_fusion.3
  279.9 2.6 maximum_bitcast_fusion.3
  286.3 2.6 maximum_bitcast_fusion.3
  292.7 2.6 maximum_bitcast_fusion.3
  299.0 2.6 maximum_bitcast_fusion.3
  305.4 2.6 maximum_bitcast_fusion.3
  311.8 2.6 maximum_bitcast_fusion.3
  318.1 2.6 maximum_bitcast_fusion.3
  325.6 32.4 %reduce-scatter.2.cloned.1.call-done = bf16[16,8192]{1,0:T(8,128)(2,1)} async-done(((bf16[64,8192]{1,0:T(8,128)(2,1)}), bf16[16,8192]{1,0:T(8,128)(2,1)}) %reduce-scatter.2.cloned.1.call-update) | async-done | bytes 262160 | tf_op jit(solution)/shard_map/reduce_scatter | solution.py:118
  (115 shorter events, 61.6 us)
Async XLA Ops:
  6.5 7.4 %copy-start.3 = (f32[32]{0:T(128)S(1)}, f32[32]{0:T(128)}, u32[]{:S(2)}) copy-start(f32[32]{0:T(128)} %constant.54.clone) | copy-start | bytes 388
  6.5 6.0 %copy-start.2 = (bf16[64,16]{0,1:T(8,128)(2,1)S(1)}, bf16[64,16]{0,1:T(8,128)(2,1)}, u32[]{:S(2)}) copy-start(bf16[64,16]{0,1:T(8,128)(2,1)} %param.15) | copy-start | bytes 6148
  6.5 215.3 %all-gather.3.cloned.1.call-start = ((), (), s32[]{:S(2)}) async-start(), calls=%async_computation.2 | async-start | bytes 2113536 | tf_op jit(solution)/shard_map/all_gather | solution.py:96
  11.2 346.8 %reduce-scatter.2.cloned.1.call-start = ((), (), s32[]{:S(2)}) async-start(), calls=%async_computation.1 | async-start | bytes 1310720 | tf_op jit(solution)/shard_map/reduce_scatter | solution.py:118
  221.9 0.7 copy-start.1
  324.6 1.0 copy-start
Sparse Core Ops, SparseCore 0:
  11.8 209.9 all-gather.2
  325.7 32.2 reduce-scatter.1
where the time goes:
time: 368 us; the launch traced here: 367 us
  waiting for transfers between devices  240 us (65%)
  local copies, waits for them, and re-layouts  44 us (12%)
  matrix products  42.2 us (11%)
  other arithmetic  25.3 us (7%)
  between operations  14.7 us (4%)
    all_gather x1, waiting for transfers between devices, on_device(): piece = lax.all_gather(k_rot, 'ctx', axis=0, tiled=True)  207 us
    dot_general x16, matrix products, tile_scores(): lax.dot_general(q_block.reshape(rows_here * heads_here, DH), k_block, (((...  42.2 us
    reduce_scatter x1, waiting for transfers between devices, on_device(): lax.psum_scatter(partials, 'head', scatter_dimension=0, tiled=True)  32.4 us
    max x16, local copies, waits for them, and re-layouts, tile_scores(): jnp.maximum(raw, 0.0)  30.7 us
    add x16, other arithmetic, one_block(): return score_block(k_block, offset + jnp.arange(block_len, dtype=jnp.int32))  9.88 us
    dynamic_slice x16, local copies, waits for them, and re-layouts, compute(): tiles = lax.map(one_block, (stacked, offsets))  9.55 us
    reduce_sum x16, other arithmetic, tile_scores(): jnp.sum(active * weights.reshape(rows_here, groups, heads_here // groups,...  7.39 us
  transfers between devices with their start and end apart: 2, of which 2 were waited for; matrix products, arithmetic and copies ran while one was open for 1% of the time, Pallas kernels for 0%

commit v1 on v0

--- a/solution.py
+++ b/solution.py
@@ -93,7 +93,9 @@
         parts = tile_scores(q_rot, rows_w, k_block, groups, row_glob, row_doc, key_glob)
         return parts[:, 0, :]
 
-    piece = lax.all_gather(k_rot, "ctx", axis=0, tiled=True)
+    piece = jnp.concatenate(
+        lax.all_to_all(jnp.stack([k_rot] * lax.axis_size("ctx")), "ctx", 0, 0), axis=0
+    )
     start = jnp.int32(0)
     piece_len = piece.shape[0]
     block_len = math.gcd(piece_len, 512)

time: 368 us -> 269 us (0.73)
  waiting for transfers between devices: 240 us -> 116 us
  starting transfers between devices: 0.04 us -> 23.7 us
    all_gather x1 -> x0, waiting for transfers between devices: 207 us -> none  [on_device(): piece = lax.all_gather(k_rot, 'ctx', axis=0, tiled=True)]
    all_to_all x0 -> x1, waiting for transfers between devices: none -> 90.2 us  [on_device(): lax.all_to_all(jnp.stack([k_rot] * lax.axis_size('ctx')), 'ctx', 0, 0)]
    all_to_all x0 -> x1, starting transfers between devices: none -> 23.6 us  [on_device(): lax.all_to_all(jnp.stack([k_rot] * lax.axis_size('ctx')), 'ctx', 0, 0)]
    reduce_scatter x1, waiting for transfers between devices: 32.4 us -> 26.1 us  [on_device(): lax.psum_scatter(partials, 'head', scatter_dimension=0, tiled=True)]
  transfers between devices with their start and end apart: 2 -> 2, of which waited for: 2 -> 2; matrix products, arithmetic and copies ran while one was open for 1% -> 0% of each run, Pallas kernels for 0% -> 0%
where the time goes in v1:
time: 269 us; the launch traced here: 267 us
  waiting for transfers between devices  116 us (43%)
  local copies, waits for them, and re-layouts  45.5 us (17%)
  matrix products  42.2 us (16%)
  other arithmetic  24.3 us (9%)
  starting transfers between devices  23.7 us (9%)
  between operations  14.8 us (6%)
    all_to_all x1, waiting for transfers between devices, on_device(): lax.all_to_all(jnp.stack([k_rot] * lax.axis_size('ctx')), 'ctx', 0, 0)  90.2 us
    dot_general x16, matrix products, tile_scores(): lax.dot_general(q_block.reshape(rows_here * heads_here, DH), k_block, (((...  42.2 us
    max x16, local copies, waits for them, and re-layouts, tile_scores(): jnp.maximum(raw, 0.0)  30.7 us
    reduce_scatter x1, waiting for transfers between devices, on_device(): lax.psum_scatter(partials, 'head', scatter_dimension=0, tiled=True)  26.1 us
    all_to_all x1, starting transfers between devices, on_device(): lax.all_to_all(jnp.stack([k_rot] * lax.axis_size('ctx')), 'ctx', 0, 0)  23.6 us
    add x16, other arithmetic, one_block(): return score_block(k_block, offset + jnp.arange(block_len, dtype=jnp.int32))  9.88 us
    dynamic_slice x16, local copies, waits for them, and re-layouts, compute(): tiles = lax.map(one_block, (stacked, offsets))  9.55 us
    reduce_sum x16, other arithmetic, tile_scores(): jnp.sum(active * weights.reshape(rows_here, groups, heads_here // groups,...  7.39 us
  transfers between devices with their start and end apart: 2, of which 2 were waited for; matrix products, arithmetic and copies ran while one was open for 0% of the time, Pallas kernels for 0%

profile of v1, /device:TPU:1, one launch (start us, length us, event | category | flops | bytes accessed | tf_op | source)
XLA Modules:
  0.0 267.5 jit_solution(9604627888449642586)
XLA Ops:
  12.4 23.6 %all-to-all-start = ((bf16[128,64,128]{2,1,0:T(8,128)(2,1)}), bf16[128,64,128]{2,1,0:T(8,128)(2,1)}, u32[]{:S(2)}, u32[]{:S(2)}) async-start(bf16[128,64,128]{2,1,0:T(8,128)(2,1)} %stack.2), calls=%async_computation | async-start | bytes 4194304 | tf_op jit(solution)/shard_map/all_to_all | solution.py:97
  38.8 90.2 %all-to-all-done = bf16[128,64,128]{2,1,0:T(8,128)(2,1)} async-done(((bf16[128,64,128]{2,1,0:T(8,128)(2,1)}), bf16[128,64,128]{2,1,0:T(8,128)(2,1)}, u32[]{:S(2)}, u32[]{:S(2)}) %all-to-all-start) | async-done | bytes 2097184 | tf_op jit(solution)/shard_map/all_to_all | solution.py:97
  129.0 102.7 %conditional.1 = (bf16[64,8192]{1,0:T(8,128)(2,1)S(1)}) conditional(s32[]{:T(128)} %convert_element_type.42, () %tuple.18, (bf16[128,64,128]{2,1,0:T(8,128)(2,1)}, bf16[64,16,128]{2,1,0:T(8,128)(2,1)S(1)}, f32[64,16]{1,0:T(8,128)S(1)}, s32[64]{0:T(128)S(1)}, s32[64]{0:T(128)S(1)}) %tuple.19), branch_computations={%region_4.0_spmd, %region_5.9_spmd} | conditional | flops 135890448 | bytes 13190965 | solution.py:119
  129.7 101.8 %while.13 = (s32[]{:T(128)}, bf16[16,64,512]{2,1,0:T(8,128)(2,1)S(1)}, s32[16]{0:T(128)S(1)}, s32[64]{0:T(128)S(1)}, s32[64]{0:T(128)S(1)}, /*index=5*/bf16[16,5...) while((s32[]{:T(128)}, ...), condition=%wide.wide.region_8.8_spmd, body=%wide.wide.region_6.7_spmd.sunk | while | flops 135889408 | bytes 8988281 | solution.py:112
  129.7 2.6 maximum_bitcast_fusion.4
  132.4 1.9 copy.25
  136.1 2.6 maximum_bitcast_fusion.4
  138.7 1.9 copy.25
  142.5 2.6 maximum_bitcast_fusion.4
  145.1 1.9 copy.25
  148.8 2.6 maximum_bitcast_fusion.4
  155.2 2.6 maximum_bitcast_fusion.4
  161.6 2.6 maximum_bitcast_fusion.4
  167.9 2.6 maximum_bitcast_fusion.4
  174.3 2.6 maximum_bitcast_fusion.4
  180.7 2.6 maximum_bitcast_fusion.4
  187.0 2.6 maximum_bitcast_fusion.4
  193.4 2.6 maximum_bitcast_fusion.4
  199.8 2.6 maximum_bitcast_fusion.4
  206.1 2.6 maximum_bitcast_fusion.4
  212.5 2.6 maximum_bitcast_fusion.4
  218.9 2.6 maximum_bitcast_fusion.4
  225.2 2.6 maximum_bitcast_fusion.4
  232.7 26.1 %reduce-scatter.2.cloned.1.call-done = bf16[16,8192]{1,0:T(8,128)(2,1)} async-done(((bf16[64,8192]{1,0:T(8,128)(2,1)}), bf16[16,8192]{1,0:T(8,128)(2,1)}) %reduce-scatter.2.cloned.1.call-update) | async-done | bytes 262160 | tf_op jit(solution)/shard_map/reduce_scatter | solution.py:120
  (117 shorter events, 64.0 us)
Async XLA Ops:
  12.4 23.7 %copy-start.2 = (bf16[64,2048]{1,0:T(8,128)(2,1)S(1)}, bf16[64,2048]{1,0:T(8,128)(2,1)}, u32[]{:S(2)}) copy-start(bf16[64,2048]{1,0:T(8,128)(2,1)} %param.11) | copy-start | bytes 786436
  12.4 116.6 %all-to-all-start = ((bf16[128,64,128]{2,1,0:T(8,128)(2,1)}), bf16[128,64,128]{2,1,0:T(8,128)(2,1)}, u32[]{:S(2)}, u32[]{:S(2)}) async-start(bf16[128,64,128]{2,1,0:T(8,128)(2,1)} %stack.2), calls=%async_computation | async-start | bytes 4194304 | tf_op jit(solution)/shard_map/all_to_all | solution.py:97
  36.0 0.7 copy-start.3
  36.0 2.1 copy-start.4
  36.0 222.8 %reduce-scatter.2.cloned.1.call-start = ((), (), s32[]{:S(2)}) async-start(), calls=%async_computation.2 | async-start | bytes 1310720 | tf_op jit(solution)/shard_map/reduce_scatter | solution.py:120
  129.0 0.7 copy-start.1
  231.7 1.0 copy-start
Sparse Core Ops, SparseCore 0:
  232.8 25.9 reduce-scatter.1
